TPU v7x, 32 devices: a whole 2x2x4 slice. The times are simulated.
32 devices in a mesh: group: 4 (over y, x), member: 8 (over z, core).
Axes of the slice: x: 2, y: 2, z: 4, core: 2. Of those that a mesh axis runs over, the one named last changes fastest.
Arguments:
- amplitudes: bfloat16 [512, 128, 128], P(('group', 'member')), may hold values from -6 to 6
- integrals: bfloat16 [256, 128, 128], P(('group', 'member')), may hold values from -0.02734375 to 0.02734375
- tasks: int32 [12288, 3], P(('group', 'member')), may hold values from 0 to 15, as said below
- requests: int32 [128, 4], P(('group', 'member')), may hold values from 0 to 7
- counts: int32 [32], P(('group', 'member')), may hold values from 1 to 384, as said below
Outputs:
- residual: float32 [32, 128, 128], P(('group', 'member'))
Inputs may be any that keep to these rules, and one draw needn't show every extreme that they name: `tasks`: column 0 is below 16, column 1 below 16, column 2 below 8; slots beyond a device's count hold valid entries too. `counts`: some device has 384 live tasks in every draw.
All inputs are finite; a program needn't handle non-finite values.
Results may differ from a plain program's by a relative error of at most 0.0003.
Values may be sent and summed in bfloat16 or wider, within the bound.
A program may use at most 64 MiB of HBM per device.

v0:
```python
import functools

import jax
import jax.numpy as jnp
from jax import lax
from jax.experimental import pallas as pl
from jax.experimental.pallas import tpu as pltpu
from jax.sharding import PartitionSpec as P

RES_DEV = 1
BLOCK = 8
UNROLL = 8
MESH = pl.DeviceIdType.MESH


def round_up(n, k):
    return (n + k - 1) // k * k


def sort_tasks(n_res, n_blocks, n_amps, n_fetched, count, task_ref, slot_ref, last_ref):
    cap = task_ref.shape[1]
    slots = slot_ref.shape[1]
    valid = lax.broadcasted_iota(jnp.int32, (n_res, cap), 1) < count
    rows = lax.broadcasted_iota(jnp.int32, (n_res, cap), 0)
    hit = jnp.where(valid & (rows == task_ref[2:3, :]), 1.0, 0.0)
    upper = jnp.where(
        lax.broadcasted_iota(jnp.int32, (cap, cap), 0) <= lax.broadcasted_iota(jnp.int32, (cap, cap), 1), 1.0, 0.0
    ).astype(jnp.bfloat16)
    rank = jnp.dot(hit.astype(jnp.bfloat16), upper, preferred_element_type=jnp.float32)
    number = jnp.sum(hit, axis=1, keepdims=True).astype(jnp.int32)
    blocks = jnp.maximum((number + (BLOCK - 1)) // BLOCK, 1)
    blocks = jnp.broadcast_to(blocks, (n_res, 128))
    lower = jnp.where(
        lax.broadcasted_iota(jnp.int32, (n_res, n_res), 1) < lax.broadcasted_iota(jnp.int32, (n_res, n_res), 0), 1.0, 0.0
    ).astype(jnp.bfloat16)
    first = jnp.dot(
        lower, blocks.astype(jnp.float32).astype(jnp.bfloat16), preferred_element_type=jnp.float32
    ).astype(jnp.int32)
    last_ref[...] = jnp.clip(first + blocks - 1, 0, n_blocks - 1)
    place = jnp.sum(hit * (rank + (first[:, :1] * BLOCK).astype(jnp.float32)), axis=0, keepdims=True) - 1.0
    place = place.astype(jnp.int32)
    chosen = jnp.where(lax.broadcasted_iota(jnp.int32, (slots, cap), 0) == place, 1.0, 0.0).astype(jnp.bfloat16)
    line = lax.broadcasted_iota(jnp.int32, (8, cap), 0)
    values = jnp.where(line == 0, task_ref[0:1, :] + 1, jnp.where(line == 1, task_ref[1:2, :], 0))
    picked = lax.dot_general(
        values.astype(jnp.float32).astype(jnp.bfloat16),
        chosen,
        (((1,), (1,)), ((), ())),
        preferred_element_type=jnp.float32,
    ).astype(jnp.int32)
    starts = jnp.sum(jnp.where(lax.broadcasted_iota(jnp.int32, (n_res, 128), 1) == first, 1, 0), axis=0, keepdims=True)
    keep = jnp.concatenate([1 - starts, jnp.zeros((1, slots - 128), jnp.int32)], axis=1)
    picked = jnp.clip(picked, 0, jnp.where(lax.broadcasted_iota(jnp.int32, (8, slots), 0) == 0, n_amps, n_fetched - 1))
    slot_ref[...] = jnp.where(lax.broadcasted_iota(jnp.int32, (8, slots), 0) == 2, keep, picked)


def main_kernel(
    n_group, n_member, n_blocks,
    request_hbm, task_hbm, count_hbm, amp_hbm, int_hbm, out_ref,
    request_ref, task_ref, count_ref, slot_vmem, last_vmem, slot_ref, last_ref, amps, ints, fetched, outgoing, wanted, running, half, half_in, pair, pair_in,
    local_sem, req_send, req_recv, tile_send, tile_recv, half_send, half_recv, pair_send, pair_recv,
):
    g = lax.axis_index("group")
    m = lax.axis_index("member")
    n_z = n_member // 2
    z, core = m // 2, m % 2
    fetch_cap = request_ref.shape[1]
    tile = amps.shape[1]
    amp_copy = pltpu.make_async_copy(amp_hbm, amps.at[pl.ds(1, amp_hbm.shape[0])], local_sem.at[0])
    int_copy = pltpu.make_async_copy(int_hbm, ints, local_sem.at[1])
    request_copy = pltpu.make_async_copy(request_hbm, request_ref, local_sem.at[2])
    task_copy = pltpu.make_async_copy(task_hbm, task_ref, local_sem.at[3])
    count_copy = pltpu.make_async_copy(count_hbm, count_ref, local_sem.at[4])
    for copy in (request_copy, int_copy, task_copy, count_copy, amp_copy):
        copy.start()
    group_peers = [((g + i) % n_group, m) for i in range(1, n_group)]
    sibling = (g, z * 2 + 1 - core)
    z_peers = [(g, ((z + i) % n_z) * 2 + core) for i in range(1, n_z)]

    barrier = pltpu.get_barrier_semaphore()
    for peer in group_peers + [sibling] + z_peers:
        pl.semaphore_signal(barrier, inc=1, device_id=peer, device_id_type=MESH)
    amps[0] = jnp.zeros((tile, tile), amps.dtype)
    request_copy.wait()
    pl.semaphore_wait(barrier, n_group + n_z - 1)

    asks = []
    for i, peer in enumerate(group_peers):
        ask = pltpu.make_async_remote_copy(
            src_ref=request_ref, dst_ref=wanted.at[i], send_sem=req_send.at[i], recv_sem=req_recv.at[i],
            device_id=peer, device_id_type=MESH,
        )
        ask.start()
        asks.append(ask)
    int_copy.wait()
    for c in range(fetch_cap):
        fetched[g * fetch_cap + c] = ints[request_ref[g, c]]
    sends = []
    for i in range(n_group - 1):
        asks[i].wait_recv()
        for c in range(fetch_cap):
            outgoing[i, c] = ints[wanted[i, g, c]]
        send = pltpu.make_async_remote_copy(
            src_ref=outgoing.at[i], dst_ref=fetched.at[pl.ds(g * fetch_cap, fetch_cap)],
            send_sem=tile_send.at[i], recv_sem=tile_recv.at[i],
            device_id=((g + n_group - i - 1) % n_group, m), device_id_type=MESH,
        )
        send.start()
        sends.append(send)
    count_copy.wait()
    task_copy.wait()
    sort_tasks(
        n_member * RES_DEV, n_blocks, amp_hbm.shape[0], fetched.shape[0], count_ref[0], task_ref, slot_vmem, last_vmem,
    )
    slot_copy = pltpu.make_async_copy(slot_vmem, slot_ref, local_sem.at[5])
    last_copy = pltpu.make_async_copy(last_vmem, last_ref, local_sem.at[6])
    slot_copy.start()
    last_copy.start()
    amp_copy.wait()
    slot_copy.wait()
    last_copy.wait()
    for i in range(n_group - 1):
        asks[i].wait_send()
        source = (g + i + 1) % n_group
        pltpu.make_async_remote_copy(
            src_ref=outgoing.at[i], dst_ref=fetched.at[pl.ds(source * fetch_cap, fetch_cap)],
            send_sem=tile_send.at[i], recv_sem=tile_recv.at[i],
            device_id=group_peers[i], device_id_type=MESH,
        ).wait_recv()

    def block(b, total):
        for u in range(UNROLL):
            total = one_block(b * UNROLL + u, total)
        return total

    def one_block(b, total):
        left = []
        right = []
        for t in range(BLOCK):
            left.append(amps[slot_ref[0, b * BLOCK + t]])
            right.append(fetched[slot_ref[1, b * BLOCK + t]])
        product = jnp.dot(
            jnp.concatenate(left, axis=1), jnp.concatenate(right, axis=0), preferred_element_type=jnp.float32
        )
        total = jnp.where(slot_ref[2, b] != 0, total, 0.0) + product
        running[b] = total
        return total

    lax.fori_loop(0, n_blocks // UNROLL, block, jnp.zeros((tile, tile), jnp.float32))

    for k in range(n_z):
        half[k] = running[last_ref[2 * k + 1 - core, 0]]
    swap = pltpu.make_async_remote_copy(
        src_ref=half, dst_ref=half_in, send_sem=half_send, recv_sem=half_recv,
        device_id=sibling, device_id_type=MESH,
    )
    swap.start()
    swap.wait_recv()
    parts = []
    for i in range(1, n_z):
        k = (z + i) % n_z
        pair[i - 1] = running[last_ref[2 * k + core, 0]] + half_in[k]
        part = pltpu.make_async_remote_copy(
            src_ref=pair.at[i - 1], dst_ref=pair_in.at[i - 1],
            send_sem=pair_send.at[i - 1], recv_sem=pair_recv.at[i - 1],
            device_id=z_peers[i - 1], device_id_type=MESH,
        )
        part.start()
        parts.append(part)
    result = running[last_ref[m, 0]] + half_in[z]
    for i in range(n_z - 1):
        parts[i].wait_recv()
        result = result + pair_in[i]
    out_ref[0] = result
    swap.wait_send()
    for copy in sends + parts:
        copy.wait_send()


def per_device(amplitudes, integrals, tasks, requests, counts):
    tile = amplitudes.shape[1]
    n_group = lax.axis_size("group")
    n_member = lax.axis_size("member")
    n_res = RES_DEV * n_member
    cap = tasks.shape[0]
    fetch_cap = requests.shape[1]
    n_z = n_member // 2
    n_blocks = round_up((cap + BLOCK - 1) // BLOCK + n_res, UNROLL)
    slots = round_up(n_blocks * BLOCK, 128)
    vmem = pl.BlockSpec(memory_space=pltpu.VMEM)
    hbm = pl.BlockSpec(memory_space=pltpu.HBM)
    f32, bf16 = jnp.float32, amplitudes.dtype
    dma = pltpu.SemaphoreType.DMA
    return pl.pallas_call(
        functools.partial(main_kernel, n_group, n_member, n_blocks),
        out_shape=jax.ShapeDtypeStruct((RES_DEV, tile, tile), f32),
        in_specs=[hbm] * 5,
        out_specs=vmem,
        scratch_shapes=[
            pltpu.SMEM(requests.shape, jnp.int32),
            pltpu.VMEM((tasks.shape[1], cap), jnp.int32),
            pltpu.SMEM(counts.shape, jnp.int32),
            pltpu.VMEM((8, slots), jnp.int32),
            pltpu.VMEM((n_res, 128), jnp.int32),
            pltpu.SMEM((8, slots), jnp.int32),
            pltpu.SMEM((n_res, 128), jnp.int32),
            pltpu.VMEM((amplitudes.shape[0] + 1, tile, tile), bf16),
            pltpu.VMEM(integrals.shape, bf16),
            pltpu.VMEM((n_group * fetch_cap, tile, tile), bf16),
            pltpu.VMEM((n_group - 1, fetch_cap, tile, tile), bf16),
            pltpu.SMEM((n_group - 1,) + requests.shape, jnp.int32),
            pltpu.VMEM((n_blocks, tile, tile), f32),
            pltpu.VMEM((n_z, tile, tile), f32),
            pltpu.VMEM((n_z, tile, tile), f32),
            pltpu.VMEM((n_z - 1, tile, tile), f32),
            pltpu.VMEM((n_z - 1, tile, tile), f32),
            dma((7,)),
            dma((n_group - 1,)),
            dma((n_group - 1,)),
            dma((n_group - 1,)),
            dma((n_group - 1,)),
            dma,
            dma,
            dma((n_z - 1,)),
            dma((n_z - 1,)),
        ],
        compiler_params=pltpu.CompilerParams(
            collective_id=0, has_side_effects=True, vmem_limit_bytes=67043328
        ),
    )(requests, tasks.T, counts, amplitudes, integrals)


def solution(mesh):
    return jax.shard_map(
        per_device,
        mesh=mesh,
        in_specs=(
            P(("group", "member"), None, None),
            P(("group", "member"), None, None),
            P(("group", "member"), None),
            P(("group", "member"), None),
            P(("group", "member")),
        ),
        out_specs=P(("group", "member"), None, None),
        check_vma=False,
    )
```

profile of v0, /device:TPU:1, one launch (start us, length us, event | category | flops | bytes accessed | tf_op | source)
XLA Modules:
  0.0 29.0 jit_solution(1243446766716397813)
XLA Ops:
  0.7 26.8 %shard_map.55 = f32[1,128,128]{2,1,0:T(8,128)} custom-call(s32[4,4]{1,0:T(4,128)} %request_hbm.1, s32[3,384]{1,0:T(4,128)} %bitcast.1, s32[1]{0:T(128)S(6)} %copy.7.count_hbm, bf16[16,128,128]{2,1,0:T(8,128)(2,1)} %amp_hbm.1, bf16[8,128,128]{2,1,0:T(8,128)(2,1)} %int_hbm.1), custom_call_target="tpu_custom_call" | custom-call | tf_op jit(solution)/shard_map/pallas_call | solution.py:194
  27.5 1.5 %copy.8 = f32[1,128,128]{2,1,0:T(8,128)} copy(f32[1,128,128]{2,1,0:T(8,128)} %shard_map.55) | data formatting | bytes 131072
where the time goes:
time: 29.1 us; the launch traced here: 29 us
  Pallas kernels  26.8 us (92%)
  local copies, waits for them, and re-layouts  1.47 us (5%)
  between operations  0.66 us (2%)
    pallas_call x1, Pallas kernels, per_device(): pl.pallas_call(functools.partial(main_kernel, n_group, n_member, n_blocks...  26.8 us
    unnamed x1, local copies, waits for them, and re-layouts  1.47 us

commit v1 on v0

--- a/solution.py
+++ b/solution.py
@@ -177,7 +177,7 @@
         copy.wait_send()
 
 
-def per_device(amplitudes, integrals, tasks, requests, counts):
+def sorted_tasks_call(amplitudes, integrals, tasks, requests, counts):
     tile = amplitudes.shape[1]
     n_group = lax.axis_size("group")
     n_member = lax.axis_size("member")
@@ -230,6 +230,343 @@
     )(requests, tasks.T, counts, amplitudes, integrals)
 
 
+SUB = 8
+CODES = 32767.0
+
+
+def count_weights(n_bins, n_res, n_amps, parts, count, task_ref, e_ref, row_ref):
+    cap = task_ref.shape[1]
+    width = parts * n_amps * SUB
+    share = -(-cap // parts)
+    bins = task_ref[1:2, :] * n_res + task_ref[2:3, :]
+    lane = lax.broadcasted_iota(jnp.int32, (1, cap), 1)
+    amp = task_ref[0:1, :]
+    for p in range(1, parts):
+        amp = amp + jnp.where(lane >= p * share, n_amps, 0)
+    hit_bin = (lax.broadcasted_iota(jnp.int32, (n_bins, cap), 0) == bins) & (
+        lax.broadcasted_iota(jnp.int32, (n_bins, cap), 1) < count
+    )
+    first = amp * SUB
+    rows = lax.broadcasted_iota(jnp.int32, (width, cap), 0)
+    hit_amp = (rows >= first) & (rows < first + SUB)
+    row_ref[...] = lax.dot_general(
+        jnp.where(hit_bin, 1.0, 0.0).astype(jnp.bfloat16),
+        jnp.where(hit_amp, 1.0, 0.0).astype(jnp.bfloat16),
+        (((1,), (1,)), ((), ())),
+        preferred_element_type=jnp.float32,
+    )
+    same = jnp.where(
+        lax.broadcasted_iota(jnp.int32, (SUB, width), 1) % SUB
+        == lax.broadcasted_iota(jnp.int32, (SUB, width), 0),
+        1.0, 0.0,
+    )
+    for b in range(0, n_bins, 2):
+        pair = [jnp.broadcast_to(row_ref[b + t:b + t + 1, :], (SUB, width)) * same for t in range(2)]
+        e_ref[b * SUB:(b + 2) * SUB, :] = jnp.concatenate(pair, axis=0).astype(jnp.bfloat16)
+
+
+def combine_amps(n_group, n_res, fetch_cap, parts, amps, e_ref, hi_ref, lo_ref):
+    n_amps, tile = amps.shape[0], amps.shape[1]
+    block = fetch_cap * n_res * SUB
+
+    def rows16(q, carry):
+        base = pl.multiple_of(q * 2 * SUB, 2 * SUB)
+        rows = amps[:, pl.ds(base, 2 * SUB), :].astype(jnp.float32)
+        halves = [
+            rows[:, t * SUB:(t + 1) * SUB, :].reshape(n_amps * SUB, tile).astype(jnp.bfloat16) for t in range(2)
+        ]
+        right = jnp.concatenate(halves, axis=1)
+        right = jnp.concatenate([right] * parts, axis=0)
+        for h in range(n_group):
+            made = jnp.dot(e_ref[h * block:(h + 1) * block, :], right, preferred_element_type=jnp.float32)
+            for c in range(fetch_cap):
+                for r in range(n_res):
+                    at = (c * n_res + r) * SUB
+                    value = jnp.concatenate(
+                        [made[at:at + SUB, :tile], made[at:at + SUB, tile:]], axis=0
+                    )
+                    high = value.astype(jnp.bfloat16)
+                    low = (value - high.astype(jnp.float32)).astype(jnp.bfloat16)
+                    place = (h, pl.ds(pl.multiple_of(r * tile + base, 2 * SUB), 2 * SUB), pl.ds(c * tile, tile))
+                    hi_ref[place] = high
+                    lo_ref[place] = low
+        return carry
+
+    lax.fori_loop(0, tile // (2 * SUB), rows16, 0)
+
+
+def dense_kernel(
+    n_group, n_member, parts,
+    request_hbm, task_hbm, count_hbm, amp_hbm, int_hbm, out_ref,
+    request_ref, task_ref, count_ref, amps, ints, fetched, outgoing, wanted, row_ref, e_ref, hi_ref, lo_ref, acc,
+    half, half_in, code, code_in, scale, scale_in,
+    local_sem, far_sem, chain_sem, req_send, req_recv, tile_send, tile_recv, half_send, half_recv,
+    code_send, code_recv, scale_send, scale_recv,
+):
+    g = lax.axis_index("group")
+    m = lax.axis_index("member")
+    n_z = n_member // 2
+    n_res = n_member * RES_DEV
+    z, core = m // 2, m % 2
+    fetch_cap = request_ref.shape[1]
+    tile = amps.shape[1]
+    amp_copy = pltpu.make_async_copy(amp_hbm, amps, local_sem.at[0])
+    int_copy = pltpu.make_async_copy(int_hbm, ints, local_sem.at[1])
+    request_copy = pltpu.make_async_copy(request_hbm, request_ref, local_sem.at[2])
+    task_copy = pltpu.make_async_copy(task_hbm, task_ref, local_sem.at[3])
+    count_copy = pltpu.make_async_copy(count_hbm, count_ref, local_sem.at[4])
+    for copy in (request_copy, int_copy, task_copy, count_copy, amp_copy):
+        copy.start()
+    row, col = g // 2, g % 2
+    near = [row * 2 + 1 - col, (1 - row) * 2 + col]
+    partners = near + [(1 - row) * 2 + 1 - col]
+    sibling = (g, z * 2 + 1 - core)
+
+    barrier = pltpu.get_barrier_semaphore()
+
+    def greet(device):
+        pl.semaphore_signal(barrier, inc=1, device_id=device, device_id_type=MESH)
+
+    for h in near:
+        greet((h, m))
+    greet(sibling)
+
+    @pl.when(z > 0)
+    def _():
+        greet((g, m - 2))
+
+    @pl.when(z < n_z - 1)
+    def _():
+        greet((g, m + 2))
+
+    request_copy.wait()
+    ends = jnp.where(z > 0, 1, 0) + jnp.where(z < n_z - 1, 1, 0)
+    pl.semaphore_wait(barrier, 3 + ends)
+
+    def ask(i):
+        return pltpu.make_async_remote_copy(
+            src_ref=request_ref, dst_ref=wanted.at[i], send_sem=req_send.at[i], recv_sem=req_recv.at[i],
+            device_id=(partners[i], m), device_id_type=MESH,
+        )
+
+    def tiles(i):
+        return pltpu.make_async_remote_copy(
+            src_ref=outgoing.at[i], dst_ref=fetched.at[i + 1], send_sem=tile_send.at[i], recv_sem=tile_recv.at[i],
+            device_id=(partners[i], m), device_id_type=MESH,
+        )
+
+    ask(0).start()
+    ask(1).start()
+    pl.semaphore_signal(far_sem, inc=1, device_id=(near[0], m), device_id_type=MESH)
+    up, down = chain_sem.at[0], chain_sem.at[1]
+
+    def tell_up():
+        pl.semaphore_signal(up, inc=1, device_id=(g, m + 2), device_id_type=MESH)
+
+    def tell_down():
+        pl.semaphore_signal(down, inc=1, device_id=(g, m - 2), device_id_type=MESH)
+
+    @pl.when((z == 1) & (z < n_z - 1))
+    def _():
+        tell_up()
+
+    @pl.when((z == n_z - 2) & (z > 0))
+    def _():
+        tell_down()
+
+    count_copy.wait()
+    task_copy.wait()
+    n_bins = n_group * fetch_cap * n_res
+    pl.semaphore_wait(far_sem, 1)
+    ask(2).start()
+    count_weights(n_bins, n_res, amp_hbm.shape[0], parts, count_ref[0], task_ref, e_ref, row_ref)
+    int_copy.wait()
+    for c in range(fetch_cap):
+        fetched[0, c] = ints[request_ref[g, c]]
+    for i in range(n_group - 1):
+        ask(i).wait_recv()
+        for c in range(fetch_cap):
+            outgoing[i, c] = ints[wanted[i, g, c]]
+        tiles(i).start()
+
+    @pl.when(z > 1)
+    def _():
+        pl.semaphore_wait(up, 1)
+
+    @pl.when((z > 1) & (z < n_z - 1))
+    def _():
+        tell_up()
+
+    @pl.when(z < n_z - 2)
+    def _():
+        pl.semaphore_wait(down, 1)
+
+    @pl.when((z < n_z - 2) & (z > 0))
+    def _():
+        tell_down()
+
+    amp_copy.wait()
+    combine_amps(n_group, n_res, fetch_cap, parts, amps, e_ref, hi_ref, lo_ref)
+
+    def product(i, r):
+        h = g if i == 0 else partners[i - 1]
+        rows = pl.ds(pl.multiple_of(r * tile, tile), tile)
+        right = fetched[i].reshape(fetch_cap * tile, tile)
+        return jnp.dot(hi_ref[h, rows, :], right, preferred_element_type=jnp.float32) + jnp.dot(
+            lo_ref[h, rows, :], right, preferred_element_type=jnp.float32
+        )
+
+    for i in range(n_group - 1):
+        if i > 0:
+            tiles(i - 1).wait_recv()
+
+        def add(r, carry, i=i):
+            value = product(i, r)
+            acc[r] = value if i == 0 else acc[r] + value
+            return carry
+
+        lax.fori_loop(0, n_res, add, 0)
+    last = n_group - 1
+    tiles(last - 1).wait_recv()
+
+    low_end = z < n_z // 2
+
+    def order(t):
+        down_v = n_z - 1 - t
+        down_k = jnp.where(down_v > z, down_v, down_v - 1)
+        up_k = jnp.where(t < z, t, t + 1)
+        return jnp.where(low_end, down_k, up_k)
+
+    def swap(k):
+        return pltpu.make_async_remote_copy(
+            src_ref=half.at[k], dst_ref=half_in.at[k], send_sem=half_send.at[k], recv_sem=half_recv.at[k],
+            device_id=sibling, device_id_type=MESH,
+        )
+
+    ks = [order(t) for t in range(n_z - 1)] + [z]
+    for k in ks:
+        r = 2 * k + 1 - core
+        half[k] = acc[r] + product(last, r)
+        swap(k).start()
+    for k in ks:
+        r = 2 * k + core
+        acc[r] = acc[r] + product(last, r)
+
+    def sends(k):
+        return [
+            pltpu.make_async_remote_copy(
+                src_ref=s.at[k], dst_ref=d.at[z], send_sem=ss.at[k], recv_sem=rs.at[z],
+                device_id=(g, 2 * k + core), device_id_type=MESH,
+            )
+            for s, d, ss, rs in (
+                (scale, scale_in, scale_send, scale_recv), (code, code_in, code_send, code_recv),
+            )
+        ]
+
+    def arrivals(k):
+        return [
+            pltpu.make_async_remote_copy(
+                src_ref=s.at[k], dst_ref=d.at[k], send_sem=ss.at[k], recv_sem=rs.at[k],
+                device_id=(g, 2 * k + core), device_id_type=MESH,
+            )
+            for s, d, ss, rs in (
+                (scale, scale_in, scale_send, scale_recv), (code, code_in, code_send, code_recv),
+            )
+        ]
+
+    for k in ks[:-1]:
+        swap(k).wait_recv()
+        value = acc[2 * k + core] + half_in[k]
+        top = jnp.maximum(jnp.max(jnp.abs(value), axis=0, keepdims=True), 1e-30)
+        scale[k] = jnp.broadcast_to(top * (1.0 / CODES), (SUB, tile))
+        code[k] = jnp.round(value * (CODES / top)).astype(jnp.int32).astype(jnp.int16)
+        for copy in sends(k):
+            copy.start()
+    swap(z).wait_recv()
+    result = acc[m] + half_in[z]
+    for k in reversed(ks[:-1]):
+        for copy in arrivals(k):
+            copy.wait_recv()
+        part = code_in[k].astype(jnp.int32).astype(jnp.float32)
+        result = result + part * scale_in[k][:1, :]
+    out_ref[0] = result
+    for i in range(n_group - 1):
+        ask(i).wait_send()
+        tiles(i).wait_send()
+    for k in ks:
+        swap(k).wait_send()
+    for k in ks[:-1]:
+        for copy in sends(k):
+            copy.wait_send()
+
+
+def dense_call(amplitudes, integrals, tasks, requests, counts):
+    n_amps, tile = amplitudes.shape[0], amplitudes.shape[1]
+    n_group = lax.axis_size("group")
+    n_member = lax.axis_size("member")
+    n_res = RES_DEV * n_member
+    n_z = n_member // 2
+    cap = tasks.shape[0]
+    fetch_cap = requests.shape[1]
+    n_bins = n_group * fetch_cap * n_res
+    parts = -(-cap // 256)
+    width = parts * n_amps * SUB
+    vmem = pl.BlockSpec(memory_space=pltpu.VMEM)
+    hbm = pl.BlockSpec(memory_space=pltpu.HBM)
+    f32, bf16 = jnp.float32, amplitudes.dtype
+    dma = pltpu.SemaphoreType.DMA
+    return pl.pallas_call(
+        functools.partial(dense_kernel, n_group, n_member, parts),
+        out_shape=jax.ShapeDtypeStruct((RES_DEV, tile, tile), f32),
+        in_specs=[hbm] * 5,
+        out_specs=vmem,
+        scratch_shapes=[
+            pltpu.SMEM(requests.shape, jnp.int32),
+            pltpu.VMEM((tasks.shape[1], cap), jnp.int32),
+            pltpu.SMEM(counts.shape, jnp.int32),
+            pltpu.VMEM(amplitudes.shape, bf16),
+            pltpu.VMEM(integrals.shape, bf16),
+            pltpu.VMEM((n_group, fetch_cap, tile, tile), bf16),
+            pltpu.VMEM((n_group - 1, fetch_cap, tile, tile), bf16),
+            pltpu.SMEM((n_group - 1,) + requests.shape, jnp.int32),
+            pltpu.VMEM((n_bins, width), f32),
+            pltpu.VMEM((n_bins * SUB, width), bf16),
+            pltpu.VMEM((n_group, n_res * tile, fetch_cap * tile), bf16),
+            pltpu.VMEM((n_group, n_res * tile, fetch_cap * tile), bf16),
+            pltpu.VMEM((n_res, tile, tile), f32),
+            pltpu.VMEM((n_z, tile, tile), f32),
+            pltpu.VMEM((n_z, tile, tile), f32),
+            pltpu.VMEM((n_z, tile, tile), jnp.int16),
+            pltpu.VMEM((n_z, tile, tile), jnp.int16),
+            pltpu.VMEM((n_z, SUB, tile), f32),
+            pltpu.VMEM((n_z, SUB, tile), f32),
+            dma((5,)),
+            pltpu.SemaphoreType.REGULAR,
+            pltpu.SemaphoreType.REGULAR((2,)),
+            dma((n_group - 1,)),
+            dma((n_group - 1,)),
+            dma((n_group - 1,)),
+            dma((n_group - 1,)),
+            dma((n_z,)),
+            dma((n_z,)),
+            dma((n_z,)),
+            dma((n_z,)),
+            dma((n_z,)),
+            dma((n_z,)),
+        ],
+        compiler_params=pltpu.CompilerParams(
+            collective_id=0, has_side_effects=True, vmem_limit_bytes=50331648
+        ),
+    )(requests, tasks.T, counts, amplitudes, integrals)
+
+
+def per_device(amplitudes, integrals, tasks, requests, counts):
+    n_bins = lax.axis_size("group") * requests.shape[1] * lax.axis_size("member") * RES_DEV
+    if lax.axis_size("group") == 4 and n_bins * 2 <= tasks.shape[0]:
+        return dense_call(amplitudes, integrals, tasks, requests, counts)
+    return sorted_tasks_call(amplitudes, integrals, tasks, requests, counts)
+
+
 def solution(mesh):
     return jax.shard_map(
         per_device,

time: 29.1 us -> 28.9 us (level)
  the two profiles are of different devices: /device:TPU:1 before, /device:TPU:0 now
where the time goes in v1:
time: 28.9 us; the launch traced here: 28.6 us
  Pallas kernels  24.6 us (85%)
  local copies, waits for them, and re-layouts  3.33 us (12%)
  between operations  0.68 us (2%)
    pallas_call x1, Pallas kernels, dense_call(): pl.pallas_call(functools.partial(dense_kernel, n_group, n_member, parts),...  24.6 us
    unnamed x9, local copies, waits for them, and re-layouts  3.33 us

profile of v1, /device:TPU:0, one launch (start us, length us, event | category | flops | bytes accessed | tf_op | source)
XLA Modules:
  0.0 28.6 jit_solution(5619989269428721483)
XLA Ops:
  0.0 0.0 copy-start.3
  0.7 0.0 copy-done.3
  0.7 0.0 copy-start
  0.7 1.0 %copy-done = bf16[16,128,128]{2,1,0:T(8,128)(2,1)S(1)} copy-done((bf16[16,128,128]{2,1,0:T(8,128)(2,1)S(1)}, bf16[16,128,128]{2,1,0:T(8,128)(2,1)}, u32[]{:S(2)}) %copy-start) | copy-done | bytes 524312
  1.7 0.0 copy-start.1
  1.7 0.9 %copy-done.1 = bf16[8,128,128]{2,1,0:T(8,128)(2,1)S(1)} copy-done((bf16[8,128,128]{2,1,0:T(8,128)(2,1)S(1)}, bf16[8,128,128]{2,1,0:T(8,128)(2,1)}, u32[]{:S(2)}) %copy-start.1) | copy-done | bytes 262168
  2.7 0.0 copy-start.2
  2.7 0.7 %copy-done.2 = s32[384,3]{0,1:T(4,128)S(1)} copy-done((s32[384,3]{0,1:T(4,128)S(1)}, s32[384,3]{0,1:T(4,128)}, u32[]{:S(2)}) %copy-start.2) | copy-done | bytes 4632
  3.4 24.6 %shard_map.55 = f32[1,128,128]{2,1,0:T(8,128)S(1)} custom-call(s32[4,4]{1,0:T(4,128)S(1)} %copy-done.3, s32[3,384]{1,0:T(4,128)S(1)} %bitcast.1, s32[1]{0:T(128)S(6)} %copy.7.count_hbm, bf16[16,128,128]{2,1,0:T(8,128)(2,1)S(1)} %copy-done, bf16[8,128,128]{2,1,0:T(8,128)(2,1)S(1)} %copy-done.1), custom_call_target="tpu_custom_call" | custom-call | tf_op jit(solution)/shard_map/pallas_call | solution.py:518
  28.0 0.6 %copy.8 = f32[1,128,128]{2,1,0:T(8,128)} copy(f32[1,128,128]{2,1,0:T(8,128)S(1)} %shard_map.55) | data formatting | bytes 131072
Async XLA Ops:
  0.0 0.7 %copy-start.3 = (s32[4,4]{1,0:T(4,128)S(1)}, s32[4,4]{1,0:T(4,128)}, u32[]{:S(2)}) copy-start(s32[4,4]{1,0:T(4,128)} %request_hbm.1) | copy-start | bytes 196
  0.7 1.0 %copy-start = (bf16[16,128,128]{2,1,0:T(8,128)(2,1)S(1)}, bf16[16,128,128]{2,1,0:T(8,128)(2,1)}, u32[]{:S(2)}) copy-start(bf16[16,128,128]{2,1,0:T(8,128)(2,1)} %amp_hbm.1) | copy-start | bytes 1572868
  1.7 0.9 %copy-start.1 = (bf16[8,128,128]{2,1,0:T(8,128)(2,1)S(1)}, bf16[8,128,128]{2,1,0:T(8,128)(2,1)}, u32[]{:S(2)}) copy-start(bf16[8,128,128]{2,1,0:T(8,128)(2,1)} %int_hbm.1) | copy-start | bytes 786436
  2.7 0.7 %copy-start.2 = (s32[384,3]{0,1:T(4,128)S(1)}, s32[384,3]{0,1:T(4,128)}, u32[]{:S(2)}) copy-start(s32[384,3]{0,1:T(4,128)} %param.7) | copy-start | bytes 13828

commit v2 on v1

--- a/solution.py
+++ b/solution.py
@@ -297,8 +297,8 @@
 
 def dense_kernel(
     n_group, n_member, parts,
-    request_hbm, task_hbm, count_hbm, amp_hbm, int_hbm, out_ref,
-    request_ref, task_ref, count_ref, amps, ints, fetched, outgoing, wanted, row_ref, e_ref, hi_ref, lo_ref, acc,
+    request_hbm, task_hbm, count_ref, amp_hbm, int_hbm, out_ref,
+    request_ref, task_ref, amps, ints, fetched, outgoing, wanted, row_ref, e_ref, hi_ref, lo_ref, acc,
     half, half_in, code, code_in, scale, scale_in,
     local_sem, far_sem, chain_sem, req_send, req_recv, tile_send, tile_recv, half_send, half_recv,
     code_send, code_recv, scale_send, scale_recv,
@@ -314,8 +314,7 @@
     int_copy = pltpu.make_async_copy(int_hbm, ints, local_sem.at[1])
     request_copy = pltpu.make_async_copy(request_hbm, request_ref, local_sem.at[2])
     task_copy = pltpu.make_async_copy(task_hbm, task_ref, local_sem.at[3])
-    count_copy = pltpu.make_async_copy(count_hbm, count_ref, local_sem.at[4])
-    for copy in (request_copy, int_copy, task_copy, count_copy, amp_copy):
+    for copy in (request_copy, int_copy, task_copy, amp_copy):
         copy.start()
     row, col = g // 2, g % 2
     near = [row * 2 + 1 - col, (1 - row) * 2 + col]
@@ -374,7 +373,6 @@
     def _():
         tell_down()
 
-    count_copy.wait()
     task_copy.wait()
     n_bins = n_group * fetch_cap * n_res
     pl.semaphore_wait(far_sem, 1)
@@ -389,24 +387,18 @@
             outgoing[i, c] = ints[wanted[i, g, c]]
         tiles(i).start()
 
-    @pl.when(z > 1)
-    def _():
-        pl.semaphore_wait(up, 1)
-
-    @pl.when((z > 1) & (z < n_z - 1))
-    def _():
-        tell_up()
-
-    @pl.when(z < n_z - 2)
-    def _():
-        pl.semaphore_wait(down, 1)
-
-    @pl.when((z < n_z - 2) & (z > 0))
-    def _():
-        tell_down()
-
     amp_copy.wait()
     combine_amps(n_group, n_res, fetch_cap, parts, amps, e_ref, hi_ref, lo_ref)
+
+    @pl.when((z > 1) & (z < n_z - 1))
+    def _():
+        pl.semaphore_wait(up, 1)
+        tell_up()
+
+    @pl.when((z < n_z - 2) & (z > 0))
+    def _():
+        pl.semaphore_wait(down, 1)
+        tell_down()
 
     def product(i, r):
         h = g if i == 0 else partners[i - 1]
@@ -420,12 +412,17 @@
         if i > 0:
             tiles(i - 1).wait_recv()
 
-        def add(r, carry, i=i):
+        for r in range(n_res):
             value = product(i, r)
             acc[r] = value if i == 0 else acc[r] + value
-            return carry
-
-        lax.fori_loop(0, n_res, add, 0)
+    @pl.when((z > 1) & (z == n_z - 1))
+    def _():
+        pl.semaphore_wait(up, 1)
+
+    @pl.when((z < n_z - 2) & (z == 0))
+    def _():
+        pl.semaphore_wait(down, 1)
+
     last = n_group - 1
     tiles(last - 1).wait_recv()
 
@@ -502,6 +499,7 @@
 
 def dense_call(amplitudes, integrals, tasks, requests, counts):
     n_amps, tile = amplitudes.shape[0], amplitudes.shape[1]
+    pin = functools.partial(pltpu.with_memory_space_constraint, memory_space=pltpu.HBM)
     n_group = lax.axis_size("group")
     n_member = lax.axis_size("member")
     n_res = RES_DEV * n_member
@@ -518,12 +516,11 @@
     return pl.pallas_call(
         functools.partial(dense_kernel, n_group, n_member, parts),
         out_shape=jax.ShapeDtypeStruct((RES_DEV, tile, tile), f32),
-        in_specs=[hbm] * 5,
+        in_specs=[hbm, hbm, pl.BlockSpec(memory_space=pltpu.SMEM), hbm, hbm],
         out_specs=vmem,
         scratch_shapes=[
             pltpu.SMEM(requests.shape, jnp.int32),
             pltpu.VMEM((tasks.shape[1], cap), jnp.int32),
-            pltpu.SMEM(counts.shape, jnp.int32),
             pltpu.VMEM(amplitudes.shape, bf16),
             pltpu.VMEM(integrals.shape, bf16),
             pltpu.VMEM((n_group, fetch_cap, tile, tile), bf16),
@@ -557,7 +554,7 @@
         compiler_params=pltpu.CompilerParams(
             collective_id=0, has_side_effects=True, vmem_limit_bytes=50331648
         ),
-    )(requests, tasks.T, counts, amplitudes, integrals)
+    )(pin(requests), pin(tasks.T), counts, pin(amplitudes), pin(integrals))
 
 
 def per_device(amplitudes, integrals, tasks, requests, counts):

time: 28.9 us -> 22.6 us (0.78)
  Pallas kernels: 24.6 us -> 21.1 us
  local copies, waits for them, and re-layouts: 3.33 us -> 0.63 us
    pallas_call x1, Pallas kernels: 24.6 us -> 21.1 us  [dense_call(): pl.pallas_call(functools.partial(dense_kernel, n_group, n_member, parts),...]
    unnamed x9 -> x1, local copies, waits for them, and re-layouts: 3.33 us -> 0.63 us
where the time goes in v2:
time: 22.6 us; the launch traced here: 22.4 us
  Pallas kernels  21.1 us (93%)
  between operations  0.66 us (3%)
  local copies, waits for them, and re-layouts  0.63 us (3%)
    pallas_call x1, Pallas kernels, dense_call(): pl.pallas_call(functools.partial(dense_kernel, n_group, n_member, parts),...  21.1 us
    unnamed x1, local copies, waits for them, and re-layouts  0.63 us

profile of v2, /device:TPU:0, one launch (start us, length us, event | category | flops | bytes accessed | tf_op | source)
XLA Modules:
  0.0 22.4 jit_solution(14247851262488679288)
XLA Ops:
  0.7 21.1 %shard_map.55 = f32[1,128,128]{2,1,0:T(8,128)S(1)} custom-call(s32[4,4]{1,0:T(4,128)} %request_hbm.1, s32[3,384]{1,0:T(4,128)} %bitcast.1, s32[1]{0:T(128)S(6)} %copy.7.count_ref, bf16[16,128,128]{2,1,0:T(8,128)(2,1)} %amp_hbm.1, bf16[8,128,128]{2,1,0:T(8,128)(2,1)} %int_hbm.1), custom_call_target="tpu_custom_call" | custom-call | tf_op jit(solution)/shard_map/pallas_call | solution.py:516
  21.8 0.6 %copy.8 = f32[1,128,128]{2,1,0:T(8,128)} copy(f32[1,128,128]{2,1,0:T(8,128)S(1)} %shard_map.55) | data formatting | bytes 131072

commit v3 on v2

--- a/solution.py
+++ b/solution.py
@@ -265,7 +265,7 @@
         e_ref[b * SUB:(b + 2) * SUB, :] = jnp.concatenate(pair, axis=0).astype(jnp.bfloat16)
 
 
-def combine_amps(n_group, n_res, fetch_cap, parts, amps, e_ref, hi_ref, lo_ref):
+def combine_amps(first, end, n_group, n_res, fetch_cap, parts, amps, e_ref, hi_ref, lo_ref):
     n_amps, tile = amps.shape[0], amps.shape[1]
     block = fetch_cap * n_res * SUB
 
@@ -292,7 +292,7 @@
                     lo_ref[place] = low
         return carry
 
-    lax.fori_loop(0, tile // (2 * SUB), rows16, 0)
+    [rows16(q, 0) for q in range(first, end)]
 
 
 def dense_kernel(
@@ -348,11 +348,18 @@
             device_id=(partners[i], m), device_id_type=MESH,
         )
 
-    def tiles(i):
+    def tiles(i, first=0, end=fetch_cap, slot=None):
+        slot = i if slot is None else slot
+        part = pl.ds(first, end - first)
         return pltpu.make_async_remote_copy(
-            src_ref=outgoing.at[i], dst_ref=fetched.at[i + 1], send_sem=tile_send.at[i], recv_sem=tile_recv.at[i],
+            src_ref=outgoing.at[i, part], dst_ref=fetched.at[i + 1, part],
+            send_sem=tile_send.at[slot], recv_sem=tile_recv.at[slot],
             device_id=(partners[i], m), device_id_type=MESH,
         )
+
+    far = n_group - 2
+    split = fetch_cap // 2
+    pieces = [tiles(i) for i in range(far)] + [tiles(far, 0, split), tiles(far, split, fetch_cap, far + 1)]
 
     ask(0).start()
     ask(1).start()
@@ -375,9 +382,18 @@
 
     task_copy.wait()
     n_bins = n_group * fetch_cap * n_res
+    count_weights(n_bins, n_res, amp_hbm.shape[0], parts, count_ref[0], task_ref, e_ref, row_ref)
+    amp_copy.wait()
+    steps = tile // (2 * SUB)
+    early, middle = steps * 0 // 8, steps * 2 // 8
+
+    def combine(first, end):
+        combine_amps(first, end, n_group, n_res, fetch_cap, parts, amps, e_ref, hi_ref, lo_ref)
+
+    combine(0, early)
     pl.semaphore_wait(far_sem, 1)
     ask(2).start()
-    count_weights(n_bins, n_res, amp_hbm.shape[0], parts, count_ref[0], task_ref, e_ref, row_ref)
+    combine(early, middle)
     int_copy.wait()
     for c in range(fetch_cap):
         fetched[0, c] = ints[request_ref[g, c]]
@@ -385,10 +401,10 @@
         ask(i).wait_recv()
         for c in range(fetch_cap):
             outgoing[i, c] = ints[wanted[i, g, c]]
-        tiles(i).start()
-
-    amp_copy.wait()
-    combine_amps(n_group, n_res, fetch_cap, parts, amps, e_ref, hi_ref, lo_ref)
+        for piece in pieces[i:i + 1] if i < far else pieces[far:]:
+            piece.start()
+
+    combine(middle, steps)
 
     @pl.when((z > 1) & (z < n_z - 1))
     def _():
@@ -400,31 +416,25 @@
         pl.semaphore_wait(down, 1)
         tell_down()
 
-    def product(i, r):
+    def product(i, r, first, end):
         h = g if i == 0 else partners[i - 1]
-        rows = pl.ds(pl.multiple_of(r * tile, tile), tile)
-        right = fetched[i].reshape(fetch_cap * tile, tile)
-        return jnp.dot(hi_ref[h, rows, :], right, preferred_element_type=jnp.float32) + jnp.dot(
-            lo_ref[h, rows, :], right, preferred_element_type=jnp.float32
+        place = (h, pl.ds(pl.multiple_of(r * tile, tile), tile), pl.ds(first * tile, (end - first) * tile))
+        right = fetched[i, first:end].reshape((end - first) * tile, tile)
+        return jnp.dot(hi_ref[place], right, preferred_element_type=jnp.float32) + jnp.dot(
+            lo_ref[place], right, preferred_element_type=jnp.float32
         )
 
     for i in range(n_group - 1):
         if i > 0:
-            tiles(i - 1).wait_recv()
+            pieces[i - 1].wait_recv()
 
         for r in range(n_res):
-            value = product(i, r)
+            value = product(i, r, 0, fetch_cap)
             acc[r] = value if i == 0 else acc[r] + value
-    @pl.when((z > 1) & (z == n_z - 1))
-    def _():
-        pl.semaphore_wait(up, 1)
-
-    @pl.when((z < n_z - 2) & (z == 0))
-    def _():
-        pl.semaphore_wait(down, 1)
-
     last = n_group - 1
-    tiles(last - 1).wait_recv()
+    pieces[far].wait_recv()
+    for r in range(n_res):
+        acc[r] = acc[r] + product(last, r, 0, split)
 
     low_end = z < n_z // 2
 
@@ -441,13 +451,23 @@
         )
 
     ks = [order(t) for t in range(n_z - 1)] + [z]
+    @pl.when((z > 1) & (z == n_z - 1))
+    def _():
+        pl.semaphore_wait(up, 1)
+
+    @pl.when((z < n_z - 2) & (z == 0))
+    def _():
+        pl.semaphore_wait(down, 1)
+
+    pieces[far + 1].wait_recv()
     for k in ks:
         r = 2 * k + 1 - core
-        half[k] = acc[r] + product(last, r)
+        half[k] = acc[r] + product(last, r, split, fetch_cap)
+    for k in ks:
         swap(k).start()
     for k in ks:
         r = 2 * k + core
-        acc[r] = acc[r] + product(last, r)
+        acc[r] = acc[r] + product(last, r, split, fetch_cap)
 
     def sends(k):
         return [
@@ -489,7 +509,8 @@
     out_ref[0] = result
     for i in range(n_group - 1):
         ask(i).wait_send()
-        tiles(i).wait_send()
+    for piece in pieces:
+        piece.wait_send()
     for k in ks:
         swap(k).wait_send()
     for k in ks[:-1]:
@@ -542,8 +563,8 @@
             pltpu.SemaphoreType.REGULAR((2,)),
             dma((n_group - 1,)),
             dma((n_group - 1,)),
-            dma((n_group - 1,)),
-            dma((n_group - 1,)),
+            dma((n_group,)),
+            dma((n_group,)),
             dma((n_z,)),
             dma((n_z,)),
             dma((n_z,)),

time: 22.6 us -> 21.4 us (0.947)
  the two profiles are of different devices: /device:TPU:0 before, /device:TPU:1 now
where the time goes in v3:
time: 21.4 us; the launch traced here: 21.3 us
  Pallas kernels  20 us (93%)
  between operations  0.66 us (3%)
  local copies, waits for them, and re-layouts  0.63 us (3%)
    pallas_call x1, Pallas kernels, dense_call(): pl.pallas_call(functools.partial(dense_kernel, n_group, n_member, parts),...  20 us
    unnamed x1, local copies, waits for them, and re-layouts  0.63 us

profile of v3, /device:TPU:1, one launch (start us, length us, event | category | flops | bytes accessed | tf_op | source)
XLA Modules:
  0.0 21.3 jit_solution(235083342905495656)
XLA Ops:
  0.7 20.0 %shard_map.55 = f32[1,128,128]{2,1,0:T(8,128)S(1)} custom-call(s32[4,4]{1,0:T(4,128)} %request_hbm.1, s32[3,384]{1,0:T(4,128)} %bitcast.1, s32[1]{0:T(128)S(6)} %copy.7.count_ref, bf16[16,128,128]{2,1,0:T(8,128)(2,1)} %amp_hbm.1, bf16[8,128,128]{2,1,0:T(8,128)(2,1)} %int_hbm.1), custom_call_target="tpu_custom_call" | custom-call | tf_op jit(solution)/shard_map/pallas_call | solution.py:537
  20.6 0.6 %copy.8 = f32[1,128,128]{2,1,0:T(8,128)} copy(f32[1,128,128]{2,1,0:T(8,128)S(1)} %shard_map.55) | data formatting | bytes 131072

commit v4 on v3

--- a/solution.py
+++ b/solution.py
@@ -300,7 +300,7 @@
     request_hbm, task_hbm, count_ref, amp_hbm, int_hbm, out_ref,
     request_ref, task_ref, amps, ints, fetched, outgoing, wanted, row_ref, e_ref, hi_ref, lo_ref, acc,
     half, half_in, code, code_in, scale, scale_in,
-    local_sem, far_sem, chain_sem, req_send, req_recv, tile_send, tile_recv, half_send, half_recv,
+    local_sem, chain_sem, req_send, req_recv, tile_send, tile_recv, half_send, half_recv,
     code_send, code_recv, scale_send, scale_recv,
 ):
     g = lax.axis_index("group")
@@ -326,7 +326,7 @@
     def greet(device):
         pl.semaphore_signal(barrier, inc=1, device_id=device, device_id_type=MESH)
 
-    for h in near:
+    for h in partners:
         greet((h, m))
     greet(sibling)
 
@@ -340,7 +340,7 @@
 
     request_copy.wait()
     ends = jnp.where(z > 0, 1, 0) + jnp.where(z < n_z - 1, 1, 0)
-    pl.semaphore_wait(barrier, 3 + ends)
+    pl.semaphore_wait(barrier, n_group + ends)
 
     def ask(i):
         return pltpu.make_async_remote_copy(
@@ -363,7 +363,7 @@
 
     ask(0).start()
     ask(1).start()
-    pl.semaphore_signal(far_sem, inc=1, device_id=(near[0], m), device_id_type=MESH)
+    ask(2).start()
     up, down = chain_sem.at[0], chain_sem.at[1]
 
     def tell_up():
@@ -391,8 +391,6 @@
         combine_amps(first, end, n_group, n_res, fetch_cap, parts, amps, e_ref, hi_ref, lo_ref)
 
     combine(0, early)
-    pl.semaphore_wait(far_sem, 1)
-    ask(2).start()
     combine(early, middle)
     int_copy.wait()
     for c in range(fetch_cap):
@@ -464,10 +462,10 @@
         r = 2 * k + 1 - core
         half[k] = acc[r] + product(last, r, split, fetch_cap)
     for k in ks:
-        swap(k).start()
-    for k in ks:
         r = 2 * k + core
         acc[r] = acc[r] + product(last, r, split, fetch_cap)
+    for k in ks:
+        swap(k).start()
 
     def sends(k):
         return [
@@ -495,7 +493,7 @@
         swap(k).wait_recv()
         value = acc[2 * k + core] + half_in[k]
         top = jnp.maximum(jnp.max(jnp.abs(value), axis=0, keepdims=True), 1e-30)
-        scale[k] = jnp.broadcast_to(top * (1.0 / CODES), (SUB, tile))
+        scale[k] = top * (1.0 / CODES)
         code[k] = jnp.round(value * (CODES / top)).astype(jnp.int32).astype(jnp.int16)
         for copy in sends(k):
             copy.start()
@@ -505,7 +503,7 @@
         for copy in arrivals(k):
             copy.wait_recv()
         part = code_in[k].astype(jnp.int32).astype(jnp.float32)
-        result = result + part * scale_in[k][:1, :]
+        result = result + part * scale_in[k]
     out_ref[0] = result
     for i in range(n_group - 1):
         ask(i).wait_send()
@@ -556,10 +554,9 @@
             pltpu.VMEM((n_z, tile, tile), f32),
             pltpu.VMEM((n_z, tile, tile), jnp.int16),
             pltpu.VMEM((n_z, tile, tile), jnp.int16),
-            pltpu.VMEM((n_z, SUB, tile), f32),
-            pltpu.VMEM((n_z, SUB, tile), f32),
+            pltpu.VMEM((n_z, 1, tile), f32),
+            pltpu.VMEM((n_z, 1, tile), f32),
             dma((5,)),
-            pltpu.SemaphoreType.REGULAR,
             pltpu.SemaphoreType.REGULAR((2,)),
             dma((n_group - 1,)),
             dma((n_group - 1,)),

time: 21.4 us -> 20.9 us (0.977)
  Pallas kernels: 20 us -> 19.4 us
    pallas_call x1, Pallas kernels: 20 us -> 19.4 us  [dense_call(): pl.pallas_call(functools.partial(dense_kernel, n_group, n_member, parts),...]
where the time goes in v4:
time: 20.9 us; the launch traced here: 20.7 us
  Pallas kernels  19.4 us (93%)
  between operations  0.66 us (3%)
  local copies, waits for them, and re-layouts  0.63 us (3%)
    pallas_call x1, Pallas kernels, dense_call(): pl.pallas_call(functools.partial(dense_kernel, n_group, n_member, parts),...  19.4 us
    unnamed x1, local copies, waits for them, and re-layouts  0.63 us

profile of v4, /device:TPU:1, one launch (start us, length us, event | category | flops | bytes accessed | tf_op | source)
XLA Modules:
  0.0 20.7 jit_solution(13659603244284330943)
XLA Ops:
  0.7 19.4 %shard_map.55 = f32[1,128,128]{2,1,0:T(8,128)S(1)} custom-call(s32[4,4]{1,0:T(4,128)} %request_hbm.1, s32[3,384]{1,0:T(4,128)} %bitcast.1, s32[1]{0:T(128)S(6)} %copy.7.count_ref, bf16[16,128,128]{2,1,0:T(8,128)(2,1)} %amp_hbm.1, bf16[8,128,128]{2,1,0:T(8,128)(2,1)} %int_hbm.1), custom_call_target="tpu_custom_call" | custom-call | tf_op jit(solution)/shard_map/pallas_call | solution.py:535
  20.1 0.6 %copy.8 = f32[1,128,128]{2,1,0:T(8,128)} copy(f32[1,128,128]{2,1,0:T(8,128)S(1)} %shard_map.55) | data formatting | bytes 131072

commit v5 on v4

--- a/solution.py
+++ b/solution.py
@@ -321,6 +321,10 @@
     partners = near + [(1 - row) * 2 + 1 - col]
     sibling = (g, z * 2 + 1 - core)
 
+    def to(i):
+        return partners[i] if isinstance(i, int) else jnp.where(i == 0, partners[0], partners[1])
+
+
     barrier = pltpu.get_barrier_semaphore()
 
     def greet(device):
@@ -345,7 +349,7 @@
     def ask(i):
         return pltpu.make_async_remote_copy(
             src_ref=request_ref, dst_ref=wanted.at[i], send_sem=req_send.at[i], recv_sem=req_recv.at[i],
-            device_id=(partners[i], m), device_id_type=MESH,
+            device_id=(to(i), m), device_id_type=MESH,
         )
 
     def tiles(i, first=0, end=fetch_cap, slot=None):
@@ -354,7 +358,7 @@
         return pltpu.make_async_remote_copy(
             src_ref=outgoing.at[i, part], dst_ref=fetched.at[i + 1, part],
             send_sem=tile_send.at[slot], recv_sem=tile_recv.at[slot],
-            device_id=(partners[i], m), device_id_type=MESH,
+            device_id=(to(i), m), device_id_type=MESH,
         )
 
     far = n_group - 2
@@ -385,7 +389,7 @@
     count_weights(n_bins, n_res, amp_hbm.shape[0], parts, count_ref[0], task_ref, e_ref, row_ref)
     amp_copy.wait()
     steps = tile // (2 * SUB)
-    early, middle = steps * 0 // 8, steps * 2 // 8
+    early, middle = steps * 0 // 8, steps * 3 // 8
 
     def combine(first, end):
         combine_amps(first, end, n_group, n_res, fetch_cap, parts, amps, e_ref, hi_ref, lo_ref)
@@ -395,12 +399,18 @@
     int_copy.wait()
     for c in range(fetch_cap):
         fetched[0, c] = ints[request_ref[g, c]]
-    for i in range(n_group - 1):
-        ask(i).wait_recv()
+    def serve(i, which):
+        which.wait_recv()
         for c in range(fetch_cap):
             outgoing[i, c] = ints[wanted[i, g, c]]
-        for piece in pieces[i:i + 1] if i < far else pieces[far:]:
-            piece.start()
+
+    swapped = jnp.where((row == 1) & (col == 0), 1, 0)
+    for i in (swapped, 1 - swapped):
+        serve(i, ask(i))
+        tiles(i).start()
+    serve(far, ask(far))
+    for piece in pieces[far:]:
+        piece.start()
 
     combine(middle, steps)
 

time: 20.9 us -> 20.9 us (level)
  no operation moved by 1% of the time
where the time goes in v5:
time: 20.9 us; the launch traced here: 20.7 us
  Pallas kernels  19.4 us (93%)
  between operations  0.66 us (3%)
  local copies, waits for them, and re-layouts  0.63 us (3%)
    pallas_call x1, Pallas kernels, dense_call(): pl.pallas_call(functools.partial(dense_kernel, n_group, n_member, parts),...  19.4 us
    unnamed x1, local copies, waits for them, and re-layouts  0.63 us

profile of v5, /device:TPU:1, one launch (start us, length us, event | category | flops | bytes accessed | tf_op | source)
XLA Modules:
  0.0 20.7 jit_solution(7339003760113731115)
XLA Ops:
  0.7 19.4 %shard_map.55 = f32[1,128,128]{2,1,0:T(8,128)S(1)} custom-call(s32[4,4]{1,0:T(4,128)} %request_hbm.1, s32[3,384]{1,0:T(4,128)} %bitcast.1, s32[1]{0:T(128)S(6)} %copy.7.count_ref, bf16[16,128,128]{2,1,0:T(8,128)(2,1)} %amp_hbm.1, bf16[8,128,128]{2,1,0:T(8,128)(2,1)} %int_hbm.1), custom_call_target="tpu_custom_call" | custom-call | tf_op jit(solution)/shard_map/pallas_call | solution.py:545
  20.1 0.6 %copy.8 = f32[1,128,128]{2,1,0:T(8,128)} copy(f32[1,128,128]{2,1,0:T(8,128)S(1)} %shard_map.55) | data formatting | bytes 131072
